TPU v7x, 32 devices: a whole 2x2x4 slice. The times are simulated.
32 devices in a mesh: ctx: 16 (over z, y, x), tp: 2 (over core).
Axes of the slice: x: 2, y: 2, z: 4, core: 2. Of those that a mesh axis runs over, the one named last changes fastest.
Arguments:
- queries: bfloat16 [1024, 2560], P('ctx', 'tp'), may hold values from -100 to 100
- projected_keys: bfloat16 [1024, 512], P('ctx', 'tp'), may hold values from -30 to 30
- projected_values: bfloat16 [1024, 512], P('ctx', 'tp'), may hold values from -6 to 6
- hidden: bfloat16 [1024, 5120], P('ctx', 'tp'), may hold values from -6 to 6
- route_ids: int32 [1024, 1], P('ctx'), may hold values from 0 to 15; in each aligned block of 64 rows (0 to 63, 64 to 127, ...) at most 6 rows name the same one
- route_gain: float32 [1024], P('ctx'), may hold values from 0.25 to 1
- w_gate: bfloat16 [16, 5120, 4096], P('ctx', None, 'tp'), may hold values from -0.078125 to 0.078125
- w_up: bfloat16 [16, 5120, 4096], P('ctx', None, 'tp'), may hold values from -0.078125 to 0.078125
- w_down: bfloat16 [16, 4096, 5120], P('ctx', None, 'tp'), may hold values from -0.09375 to 0.09375
Outputs:
- attended: bfloat16 [1024, 2560], P('ctx', 'tp')
- mixed: bfloat16 [1024, 5120], P('ctx', 'tp')
Inputs may be any that keep to these rules, and one draw needn't show every extreme that they name: `route_ids`: within the rows of one device (aligned blocks of 64 rows) no expert is named more than 6 times, a bound that some block reaches.
All inputs are finite; a program needn't handle non-finite values.
Results may differ from a plain program's by a relative error of at most 0.0057.
Values may be sent and summed in bfloat16 or wider, within the bound.
No kernel may reach another device: no remote copies, remote signals or barrier semaphores. Data moves between devices by JAX's collectives and lax.ppermute only.
A program may use at most 128 MiB of HBM per device.

v0:
```python
import math
import jax
import jax.numpy as jnp
from jax import lax
from jax.sharding import PartitionSpec as P

HEAD_SIZE = 128
EXPERTS = 16
CAP = 6
masked_score = -1e30


def body(
    queries, projected_keys, projected_values, hidden, route_ids, route_gain, w_gate, w_up, w_down
):
    tok_rows = queries.shape[0]
    width_q = queries.shape[1]
    width_kv = projected_keys.shape[1]
    ctx_count = lax.axis_size("ctx")
    ctx_index = lax.axis_index("ctx")
    offsets = jnp.arange(tok_rows, dtype=jnp.int32)
    query_use, key_use, value_use = (queries, projected_keys, projected_values)

    def position(device, offset):
        return device * tok_rows + offset

    query_pos = position(ctx_index, offsets)
    query_top = jnp.max(query_pos)
    kv_heads = width_kv // HEAD_SIZE
    head_group = width_q // HEAD_SIZE // kv_heads
    query_tensor = query_use.reshape(tok_rows, kv_heads, head_group, HEAD_SIZE)
    score_scale = HEAD_SIZE ** (-0.5)
    key_whole, value_whole = (
        lax.all_gather(key_use, "ctx", axis=0, tiled=True),
        lax.all_gather(value_use, "ctx", axis=0, tiled=True),
    )
    total_rows = key_whole.shape[0]
    block_rows = math.gcd(total_rows, 1024)

    def absorb_block(block_index, state):
        block_start = block_index * block_rows
        key_block = lax.dynamic_slice_in_dim(key_whole, block_start, block_rows, 0).reshape(
            block_rows, kv_heads, HEAD_SIZE
        )
        value_block = lax.dynamic_slice_in_dim(value_whole, block_start, block_rows, 0).reshape(
            block_rows, kv_heads, HEAD_SIZE
        )
        global_rows = block_start + jnp.arange(block_rows, dtype=jnp.int32)
        key_pos = position(global_rows // tok_rows, global_rows % tok_rows)

        def update(inner_state):
            running_max, running_sum, running_out = inner_state
            scores = (
                jnp.einsum(
                    "qhgd,khd->hgqk", query_tensor, key_block, preferred_element_type=jnp.float32
                )
                * score_scale
            )
            allowed = query_pos[:, None] >= key_pos[None, :]
            scores = jnp.where(allowed, scores, masked_score)
            new_max = jnp.maximum(running_max, jnp.max(scores, axis=3))
            weights = jnp.where(allowed, jnp.exp(scores - new_max[..., None]), 0.0)
            factor = jnp.exp(running_max - new_max)
            new_sum = running_sum * factor + jnp.sum(weights, axis=3)
            partial_out = jnp.einsum(
                "hgqk,khd->qhgd",
                weights.astype(jnp.bfloat16),
                value_block,
                preferred_element_type=jnp.float32,
            )
            new_out = running_out * jnp.transpose(factor, (2, 0, 1))[..., None] + partial_out
            return (new_max, new_sum, new_out)

        def keep_state(inner_state):
            return inner_state

        return lax.cond(jnp.min(key_pos) <= query_top, update, keep_state, state)

    initial = (
        jnp.full((kv_heads, head_group, tok_rows), masked_score, jnp.float32),
        jnp.zeros((kv_heads, head_group, tok_rows), jnp.float32),
        jnp.zeros((tok_rows, kv_heads, head_group, HEAD_SIZE), jnp.float32),
    )
    running_max, running_sum, running_out = lax.fori_loop(
        0, total_rows // block_rows, absorb_block, initial
    )
    attended = (
        (running_out / jnp.transpose(running_sum, (2, 0, 1))[..., None])
        .reshape(tok_rows, width_q)
        .astype(jnp.bfloat16)
    )
    ids_flat = route_ids[:, 0]
    chosen = (ids_flat[:, None] == jnp.arange(EXPERTS, dtype=jnp.int32)[None, :]).astype(jnp.int32)
    ranking = jnp.sum((jnp.cumsum(chosen, axis=0) - chosen) * chosen, axis=1)
    slot_of = ids_flat * CAP + ranking
    selector = (jnp.arange(EXPERTS * CAP, dtype=jnp.int32)[:, None] == slot_of[None, :]).astype(
        jnp.bfloat16
    )
    host_count = ctx_count // EXPERTS
    feature_width = hidden.shape[1]
    packed = jnp.dot(selector, hidden, preferred_element_type=jnp.float32).astype(jnp.bfloat16)
    packed = jnp.broadcast_to(
        packed.reshape(EXPERTS, 1, CAP, feature_width), (EXPERTS, host_count, CAP, feature_width)
    ).reshape(ctx_count, CAP, feature_width)
    arrived = lax.all_to_all(packed, "ctx", split_axis=0, concat_axis=0, tiled=True)
    arrived = lax.all_gather(arrived, "tp", axis=2, tiled=True)
    slot_count = arrived.shape[1]
    flat_rows = arrived.reshape(-1, arrived.shape[2])
    gate_val = jnp.dot(flat_rows, w_gate[0], preferred_element_type=jnp.float32)
    up_val = jnp.dot(flat_rows, w_up[0], preferred_element_type=jnp.float32)
    inner = (jax.nn.silu(gate_val) * up_val).astype(jnp.bfloat16)
    pair_inner = lax.all_gather(inner, "tp", axis=1, tiled=True)
    partial_out = jnp.dot(pair_inner, w_down[0], preferred_element_type=jnp.float32).astype(
        jnp.bfloat16
    )
    partial_out = partial_out.reshape(ctx_count, slot_count, partial_out.shape[1])
    returned = lax.all_to_all(partial_out, "ctx", split_axis=0, concat_axis=0, tiled=True)
    out_width = returned.shape[2]
    summed = returned.reshape(EXPERTS, host_count, CAP, out_width).astype(jnp.float32).sum(axis=1)
    summed = summed.reshape(EXPERTS * CAP, out_width)
    mixed = (summed[slot_of] * route_gain[:, None]).astype(jnp.bfloat16)
    return (attended, mixed)


def solution(mesh):
    in_specs = (
        P("ctx", "tp"),
        P("ctx", "tp"),
        P("ctx", "tp"),
        P("ctx", "tp"),
        P("ctx", None),
        P("ctx"),
        P("ctx", None, "tp"),
        P("ctx", None, "tp"),
        P("ctx", None, "tp"),
    )
    out_specs = (P("ctx", "tp"), P("ctx", "tp"))
    return jax.shard_map(body, mesh=mesh, in_specs=in_specs, out_specs=out_specs, check_vma=False)
```

profile of v0, /device:TPU:0, one launch (start us, length us, event | category | flops | bytes accessed | tf_op | source)
XLA Modules:
  0.0 152.1 jit_solution(1355597205857069275)
XLA Ops:
  0.7 0.8 fusion.35
  1.5 0.8 select_reduce_fusion
  2.4 0.7 multiply_add_fusion.1
  3.0 0.3 convolution_convert_fusion
  3.3 1.0 reshape_reshape.3
  4.3 8.3 %all-to-all-start = ((bf16[16,6,2560]{2,1,0:T(8,128)(2,1)}), bf16[16,6,2560]{2,1,0:T(8,128)(2,1)S(1)}, u32[]{:S(2)}, u32[]{:S(2)}) async-start(bf16[16,6,2560]{2,1,0:T(8,128)(2,1)} %reshape_reshape.3), calls=%async_computation | async-start | bytes 1310720 | tf_op jit(solution)/shard_map/all_to_all | solution.py:105
  12.7 0.6 fusion.48
  13.3 0.6 fusion.46
  15.3 45.2 %all_gather.12 = bf16[1024,256]{1,0:T(8,128)(2,1)S(1)} all-gather(bf16[64,256]{1,0:T(8,128)(2,1)S(1)} %copy-done.4), channel_id=1, replica_groups=mesh['ctx'=16,'tp'=2] {'ctx'}, dimensions={0}, use_global_device_ids=true | all-gather | bytes 557056 | tf_op jit(solution)/shard_map/all_gather | solution.py:34
  60.5 2.7 %all_gather.14 = bf16[16,6,5120]{2,1,0:T(8,128)(2,1)S(1)} all-gather(bf16[16,6,2560]{2,1,0:T(8,128)(2,1)S(1)} %all-to-all-done), channel_id=1, replica_groups=mesh['ctx'=16,'tp'=2] {'tp'}, dimensions={2}, use_global_device_ids=true | all-gather | bytes 1474560 | tf_op jit(solution)/shard_map/all_gather | solution.py:106
  63.3 0.4 reshape.55
  63.7 8.9 %fusion.24 = f32[96,2048]{1,0:T(8,128)S(1)} fusion(bf16[96,5120]{1,0:T(8,128)(2,1)S(1)} %reshape.55, bf16[1,5120,2048]{2,1,0:T(8,128)(2,1)} %param.17), kind=kOutput, calls=%fused_computation.26 | convolution fusion | flops 2013265920 | bytes 22740992 | tf_op jit(solution)/shard_map/dot_general | solution.py:109
  72.6 11.1 %fusion.32 = bf16[96,2048]{1,0:T(8,128)(2,1)S(1)} fusion(bf16[96,5120]{1,0:T(8,128)(2,1)S(1)} %reshape.55, bf16[1,5120,2048]{2,1,0:T(8,128)(2,1)} %param.18, f32[96,2048]{1,0:T(8,128)S(1)} %fusion.24), kind=kOutput, calls=%fused_computation.31 | convolution fusion | flops 2014445568 | bytes 23134208 | tf_op jit(solution)/shard_map/dot_general | solution.py:110
  83.7 2.4 %all_gather.15 = bf16[96,4096]{1,0:T(8,128)(2,1)S(1)} all-gather(bf16[96,2048]{1,0:T(8,128)(2,1)S(1)} %fusion.32), channel_id=1, replica_groups=mesh['ctx'=16,'tp'=2] {'tp'}, dimensions={1}, use_global_device_ids=true | all-gather | bytes 1179648 | tf_op jit(solution)/shard_map/all_gather | solution.py:112
  86.2 3.4 %fusion.26 = bf16[96,2560]{1,0:T(8,128)(2,1)S(1)} fusion(bf16[96,4096]{1,0:T(8,128)(2,1)S(1)} %all_gather.15, bf16[1,4096,2560]{2,1,0:T(8,128)(2,1)S(1)} %bitcast.52), kind=kOutput, calls=%fused_computation.28 | convolution fusion | flops 2013511680 | bytes 22249472 | tf_op jit(solution)/shard_map/dot_general | solution.py:113
  89.6 1.0 reshape.56
  90.6 3.6 %all-to-all-start.1 = ((bf16[16,6,2560]{2,1,0:T(8,128)(2,1)}), bf16[16,6,2560]{2,1,0:T(8,128)(2,1)S(1)}, u32[]{:S(2)}, u32[]{:S(2)}) async-start(bf16[16,6,2560]{2,1,0:T(8,128)(2,1)} %reshape.56), calls=%async_computation.1 | async-start | bytes 1310720 | tf_op jit(solution)/shard_map/all_to_all | solution.py:117
  94.2 48.7 %all_gather.13 = bf16[1024,256]{1,0:T(8,128)(2,1)S(1)} all-gather(bf16[64,256]{1,0:T(8,128)(2,1)S(1)} %copy-done.5), channel_id=1, replica_groups=mesh['ctx'=16,'tp'=2] {'ctx'}, dimensions={0}, use_global_device_ids=true | all-gather | bytes 557056 | tf_op jit(solution)/shard_map/all_gather | solution.py:35
  142.9 6.3 %conditional.1 = ((f32[2,5,64]{2,1,0:T(8,128)S(1)}, f32[64,2,5,128]{3,0,2,1:T(8,128)S(1)})) conditional(s32[]{:T(128)} %convert_element_type.33, (f32[2,5,64]{2,1,0:T(8,128)S(1)}, f32[64,2,5,128]{3,0,2,1:T(8,128)S(1)}) %tuple.25, (s32[64]{0:T(128)S(1)}, s32[1024]{0:T(1024)S(1)}, bf16[1024,256]{1,0:T(8,128)(2,1)S(1)}, bf16[64,1280]{1,0:T(8,128)(2,1)S(1)}, ...), branch_computations={%region_2.3_spmd, %region_3.6_spmd} | conditional | flops 344295296 | bytes 22939956 | solution.py:77
  143.0 0.2 reshape.49
  143.2 0.1 reshape.48
  143.3 0.7 fusion
  144.0 1.5 copy-done.2
  145.5 0.8 fusion.2
  146.4 0.1 reshape.50
  146.5 2.6 %fusion.9 = f32[64,2,5,128]{3,0,2,1:T(8,128)S(1)} fusion(f32[2,1024,64,5]{1,2,3,0:T(8,128)} %copy-done.2, f32[2,5,64]{2,1,0:T(8,128)S(1)} %broadcast_maximum_fusion, pred[64,1024]{1,0:T(8,128)(4,1)S(1)} %broadcast_compare_fusion, bf16[1024,2,128,1]{2,1,0,3:T(2,128)(2,1)S(1)} %bitcast.53, f32[64,2,5,128]{3,0,2,1:T(8,128)S(1)} %get-tuple-element.89, ...), kind=kOutput, calls=%fused_computation.9 | convolution fusion | flops 171212800 | bytes 3871744 | tf_op jit(solution)/shard_map/while/body/eval_jaxpr/cond/branch_1_fun/hgqk,khd->qhgd/dot_general | solution.py:65
  149.1 0.2 divide_convert_fusion
  149.3 0.1 copy.19
  149.4 0.9 convert_element_type.35
  150.3 0.1 reshape.60
  150.5 0.8 gather_fusion
  151.3 0.8 multiply_convert_fusion
  (38 shorter events, 0.3 us)
Async XLA Ops:
  0.6 2.4 %copy-start = (bf16[64,2560]{1,0:T(8,128)(2,1)S(1)}, bf16[64,2560]{1,0:T(8,128)(2,1)}, u32[]{:S(2)}) copy-start(bf16[64,2560]{1,0:T(8,128)(2,1)} %param.14) | copy-start | bytes 983044
  0.6 14.6 %copy-start.4 = (bf16[64,256]{1,0:T(8,128)(2,1)S(1)}, bf16[64,256]{1,0:T(8,128)(2,1)}, u32[]{:S(2)}) copy-start(bf16[64,256]{1,0:T(8,128)(2,1)} %param.12) | copy-start | bytes 98308
  4.3 56.2 %all-to-all-start = ((bf16[16,6,2560]{2,1,0:T(8,128)(2,1)}), bf16[16,6,2560]{2,1,0:T(8,128)(2,1)S(1)}, u32[]{:S(2)}, u32[]{:S(2)}) async-start(bf16[16,6,2560]{2,1,0:T(8,128)(2,1)} %reshape_reshape.3), calls=%async_computation | async-start | bytes 1310720 | tf_op jit(solution)/shard_map/all_to_all | solution.py:105
  63.6 22.5 %slice-start = ((s8[20971520]{0:T(1024)(128)(4,1)}), s8[4194304]{0:T(1024)(128)(4,1)S(1)}, s32[]{:S(2)}) async-start(s8[20971520]{0:T(1024)(128)(4,1)} %bitcast.51), calls=%async_computation.2 | async-start | bytes 8388608
  63.6 22.5 %slice-start.1 = ((s8[20971520]{0:T(1024)(128)(4,1)}), s8[4194304]{0:T(1024)(128)(4,1)S(1)}, s32[]{:S(2)}) async-start(s8[20971520]{0:T(1024)(128)(4,1)} %bitcast.51), calls=%async_computation.3 | async-start | bytes 8388608
  63.7 22.5 %slice-start.2 = ((s8[20971520]{0:T(1024)(128)(4,1)}), s8[4194304]{0:T(1024)(128)(4,1)S(1)}, s32[]{:S(2)}) async-start(s8[20971520]{0:T(1024)(128)(4,1)} %bitcast.51), calls=%async_computation.4 | async-start | bytes 8388608
  72.6 13.5 %slice-start.3 = ((s8[20971520]{0:T(1024)(128)(4,1)}), s8[4194304]{0:T(1024)(128)(4,1)S(1)}, s32[]{:S(2)}) async-start(s8[20971520]{0:T(1024)(128)(4,1)} %bitcast.51), calls=%async_computation.5 | async-start | bytes 8388608
  72.6 13.5 %slice-start.4 = ((s8[20971520]{0:T(1024)(128)(4,1)}), s8[4194304]{0:T(1024)(128)(4,1)S(1)}, s32[]{:S(2)}) async-start(s8[20971520]{0:T(1024)(128)(4,1)} %bitcast.51), calls=%async_computation.6 | async-start | bytes 8388608
  86.2 8.1 %copy-start.5 = (bf16[64,256]{1,0:T(8,128)(2,1)S(1)}, bf16[64,256]{1,0:T(8,128)(2,1)}, u32[]{:S(2)}) copy-start(bf16[64,256]{1,0:T(8,128)(2,1)} %param.13) | copy-start | bytes 98308
  89.6 53.3 %copy-start.3 = (bf16[64,1280]{1,0:T(8,128)(2,1)S(1)}, bf16[64,1280]{1,0:T(8,128)(2,1)}, u32[]{:S(2)}) copy-start(bf16[64,1280]{1,0:T(8,128)(2,1)} %param.11) | copy-start | bytes 491524
  90.6 59.7 %all-to-all-start.1 = ((bf16[16,6,2560]{2,1,0:T(8,128)(2,1)}), bf16[16,6,2560]{2,1,0:T(8,128)(2,1)S(1)}, u32[]{:S(2)}, u32[]{:S(2)}) async-start(bf16[16,6,2560]{2,1,0:T(8,128)(2,1)} %reshape.56), calls=%async_computation.1 | async-start | bytes 1310720 | tf_op jit(solution)/shard_map/all_to_all | solution.py:117
  142.9 7.4 %copy-start.6 = (s32[64,1]{0,1:T(1,128)S(1)}, s32[64,1]{0,1:T(1,128)}, u32[]{:S(2)}) copy-start(s32[64,1]{0,1:T(1,128)} %param.15) | copy-start | bytes 772
  144.0 1.5 copy-start.2
  150.3 1.8 %copy-start.1 = (bf16[64,2560]{1,0:T(8,128)(2,1)S(1)}, bf16[64,2560]{1,0:T(8,128)(2,1)}, u32[]{:S(2)}) copy-start(bf16[64,2560]{1,0:T(8,128)(2,1)} %param.14) | copy-start | bytes 983044
  150.5 0.8 copy-start.7
where the time goes:
time: 153 us; the launch traced here: 152 us
  blocking collectives  99 us (65%)
  matrix products  27 us (18%)
  starting transfers between devices  11.9 us (8%)
  local copies, waits for them, and re-layouts  6.33 us (4%)
  other arithmetic  5.61 us (4%)
  between operations  2.2 us (1%)
    all_gather x1, blocking collectives, body(): lax.all_gather(value_use, 'ctx', axis=0, tiled=True)  48.7 us
    all_gather x1, blocking collectives, body(): lax.all_gather(key_use, 'ctx', axis=0, tiled=True)  45.2 us
    dot_general x1, matrix products, body(): up_val = jnp.dot(flat_rows, w_up[0], preferred_element_type=jnp.float32)  11.1 us
    dot_general x1, matrix products, body(): gate_val = jnp.dot(flat_rows, w_gate[0], preferred_element_type=jnp.float32)  8.92 us
    all_to_all x1, starting transfers between devices, body(): lax.all_to_all(packed, 'ctx', split_axis=0, concat_axis=0, tiled=True)  8.34 us
    all_to_all x1, starting transfers between devices, body(): lax.all_to_all(partial_out, 'ctx', split_axis=0, concat_axis=0, tiled=True)  3.59 us
    dot_general x1, matrix products, body(): jnp.dot(pair_inner, w_down[0], preferred_element_type=jnp.float32)  3.41 us
  transfers between devices with their start and end apart: 2, of which 0 were waited for; matrix products, arithmetic and copies ran while one was open for 5% of the time, Pallas kernels for 0%

commit v1 on v0

--- a/solution.py
+++ b/solution.py
@@ -8,6 +8,17 @@
 EXPERTS = 16
 CAP = 6
 masked_score = -1e30
+
+
+def cut_along(x, dim, peers):
+    before, after = (x.shape[:dim], x.shape[dim + 1 :])
+    return jnp.moveaxis(x.reshape(*before, peers, -1, *after), dim, 0)
+
+
+def laid_out(blocks, dim):
+    blocks = jnp.moveaxis(blocks, 0, dim)
+    shape = blocks.shape
+    return blocks.reshape(*shape[:dim], shape[dim] * shape[dim + 1], *shape[dim + 2 :])
 
 
 def body(
@@ -102,7 +113,14 @@
     packed = jnp.broadcast_to(
         packed.reshape(EXPERTS, 1, CAP, feature_width), (EXPERTS, host_count, CAP, feature_width)
     ).reshape(ctx_count, CAP, feature_width)
-    arrived = lax.all_to_all(packed, "ctx", split_axis=0, concat_axis=0, tiled=True)
+    count, position_2 = (lax.axis_size("ctx"), lax.axis_index("ctx"))
+    blocks = cut_along(packed, 0, count)
+    finished = [blocks[position_2]]
+    for step in range(1, count):
+        sent = blocks[(position_2 + step) % count]
+        finished.append(lax.ppermute(sent, "ctx", [(i, (i + step) % count) for i in range(count)]))
+    blocks = jnp.stack(finished)[(position_2 - jnp.arange(count)) % count]
+    arrived = laid_out(blocks, 0)
     arrived = lax.all_gather(arrived, "tp", axis=2, tiled=True)
     slot_count = arrived.shape[1]
     flat_rows = arrived.reshape(-1, arrived.shape[2])

time: 153 us -> 173 us (1.13)
  starting transfers between devices: 11.9 us -> 33.4 us
  blocking collectives: 99 us -> 96.3 us
    ppermute x0 -> x15, starting transfers between devices: none -> 26.1 us  [body(): lax.ppermute(sent, 'ctx', [(i, (i + step) % count) for i in range(count)])]
    all_to_all x1 -> x0, starting transfers between devices: 8.34 us -> none  [body(): lax.all_to_all(packed, 'ctx', split_axis=0, concat_axis=0, tiled=True)]
    all_to_all x1, starting transfers between devices: 3.59 us -> 7.3 us  [body(): lax.all_to_all(partial_out, 'ctx', split_axis=0, concat_axis=0, tiled=True)]
    all_gather x1, blocking collectives: 45.2 us -> 42.9 us  [body(): lax.all_gather(key_use, 'ctx', axis=0, tiled=True)]
  transfers between devices with their start and end apart: 2 -> 16, of which waited for: 0 -> 2; matrix products, arithmetic and copies ran while one was open for 5% -> 4% of each run, Pallas kernels for 0% -> 0%
where the time goes in v1:
time: 173 us
  blocking collectives  96.3 us (56%)
  starting transfers between devices  33.4 us (19%)
  matrix products  27 us (16%)
  local copies, waits for them, and re-layouts  6.24 us (4%)
  other arithmetic  5.58 us (3%)
  between operations  2.57 us (1%)
    all_gather x1, blocking collectives, body(): lax.all_gather(value_use, 'ctx', axis=0, tiled=True)  48.3 us
    all_gather x1, blocking collectives, body(): lax.all_gather(key_use, 'ctx', axis=0, tiled=True)  42.9 us
    ppermute x15, starting transfers between devices, body(): lax.ppermute(sent, 'ctx', [(i, (i + step) % count) for i in range(count)])  26.1 us
    dot_general x1, matrix products, body(): up_val = jnp.dot(flat_rows, w_up[0], preferred_element_type=jnp.float32)  11.1 us
    dot_general x1, matrix products, body(): gate_val = jnp.dot(flat_rows, w_gate[0], preferred_element_type=jnp.float32)  8.92 us
    all_to_all x1, starting transfers between devices, body(): lax.all_to_all(partial_out, 'ctx', split_axis=0, concat_axis=0, tiled=True)  7.3 us
  transfers between devices with their start and end apart: 16, of which 2 were waited for; matrix products, arithmetic and copies ran while one was open for 4% of the time, Pallas kernels for 0%

profile of v1, /device:TPU:0, one launch (start us, length us, event | category | flops | bytes accessed | tf_op | source)
XLA Modules:
  0.0 172.9 jit_solution(16283771299741209871)
XLA Ops:
  0.8 0.7 fusion.35
  1.7 0.8 select_reduce_fusion
  2.5 0.7 multiply_add_fusion.1
  3.8 3.0 %collective-permute-start = (bf16[1,6,2560]{2,1,0:T(8,128)(2,1)S(1)}, bf16[1,6,2560]{2,1,0:T(8,128)(2,1)S(1)}, u32[]{:S(2)}, u32[]{:S(2)}) collective-permute-start(bf16[1,6,2560]{2,1,0:T(8,128)(2,1)S(1)} %get-tuple-element.117), channel_id=1, source_target_pairs={{0,2},{2,4},{4,6},{6,8},{8,10},{10,12},{12,14},{14,16},{16,18},{18... | collective-permute-start | bytes 92168 | tf_op jit(solution)/shard_map/ppermute | solution.py:121
  6.8 1.5 collective-permute-start.1
  8.4 2.4 %collective-permute-start.2 = (bf16[1,6,2560]{2,1,0:T(8,128)(2,1)S(1)}, bf16[1,6,2560]{2,1,0:T(8,128)(2,1)S(1)}, u32[]{:S(2)}, u32[]{:S(2)}) collective-permute-start(bf16[1,6,2560]{2,1,0:T(8,128)(2,1)S(1)} %get-tuple-element.115), channel_id=1, source_target_pairs={{0,6},{2,8},{4,10},{6,12},{8,14},{10,16},{12,18},{14,20},{16,22},{... | collective-permute-start | bytes 92168 | tf_op jit(solution)/shard_map/ppermute | solution.py:121
  10.8 1.6 collective-permute-start.3
  12.4 1.6 collective-permute-start.4
  14.0 42.9 %all_gather.12 = bf16[1024,256]{1,0:T(8,128)(2,1)S(1)} all-gather(bf16[64,256]{1,0:T(8,128)(2,1)S(1)} %copy-done.4), channel_id=1, replica_groups=mesh['ctx'=16,'tp'=2] {'ctx'}, dimensions={0}, use_global_device_ids=true | all-gather | bytes 557056 | tf_op jit(solution)/shard_map/all_gather | solution.py:45
  57.6 0.6 fusion.46
  60.0 3.6 %collective-permute-start.8 = (bf16[1,6,2560]{2,1,0:T(8,128)(2,1)S(1)}, bf16[1,6,2560]{2,1,0:T(8,128)(2,1)S(1)}, u32[]{:S(2)}, u32[]{:S(2)}) collective-permute-start(bf16[1,6,2560]{2,1,0:T(8,128)(2,1)S(1)} %get-tuple-element.109), channel_id=1, source_target_pairs={{0,18},{2,20},{4,22},{6,24},{8,26},{10,28},{12,30},{14,0},{16,2},{... | collective-permute-start | bytes 92168 | tf_op jit(solution)/shard_map/ppermute | solution.py:121
  63.6 3.7 %collective-permute-start.9 = (bf16[1,6,2560]{2,1,0:T(8,128)(2,1)S(1)}, bf16[1,6,2560]{2,1,0:T(8,128)(2,1)S(1)}, u32[]{:S(2)}, u32[]{:S(2)}) collective-permute-start(bf16[1,6,2560]{2,1,0:T(8,128)(2,1)S(1)} %get-tuple-element.108), channel_id=1, source_target_pairs={{0,20},{2,22},{4,24},{6,26},{8,28},{10,30},{12,0},{14,2},{16,4},{1... | collective-permute-start | bytes 92168 | tf_op jit(solution)/shard_map/ppermute | solution.py:121
  67.5 2.5 %collective-permute-start.11 = (bf16[1,6,2560]{2,1,0:T(8,128)(2,1)S(1)}, bf16[1,6,2560]{2,1,0:T(8,128)(2,1)S(1)}, u32[]{:S(2)}, u32[]{:S(2)}) collective-permute-start(bf16[1,6,2560]{2,1,0:T(8,128)(2,1)S(1)} %get-tuple-element.106), channel_id=1, source_target_pairs={{0,24},{2,26},{4,28},{6,30},{8,0},{10,2},{12,4},{14,6},{16,8},{18,... | collective-permute-start | bytes 92168 | tf_op jit(solution)/shard_map/ppermute | solution.py:121
  70.0 2.7 %collective-permute-start.12 = (bf16[1,6,2560]{2,1,0:T(8,128)(2,1)S(1)}, bf16[1,6,2560]{2,1,0:T(8,128)(2,1)S(1)}, u32[]{:S(2)}, u32[]{:S(2)}) collective-permute-start(bf16[1,6,2560]{2,1,0:T(8,128)(2,1)S(1)} %get-tuple-element.105), channel_id=1, source_target_pairs={{0,26},{2,28},{4,30},{6,0},{8,2},{10,4},{12,6},{14,8},{16,10},{18,... | collective-permute-start | bytes 92168 | tf_op jit(solution)/shard_map/ppermute | solution.py:121
  73.3 2.4 %collective-permute-start.14 = (bf16[1,6,2560]{2,1,0:T(8,128)(2,1)S(1)}, bf16[1,6,2560]{2,1,0:T(8,128)(2,1)S(1)}, u32[]{:S(2)}, u32[]{:S(2)}) collective-permute-start(bf16[1,6,2560]{2,1,0:T(8,128)(2,1)S(1)} %get-tuple-element.103), channel_id=1, source_target_pairs={{0,30},{2,0},{4,2},{6,4},{8,6},{10,8},{12,10},{14,12},{16,14},{18,... | collective-permute-start | bytes 92168 | tf_op jit(solution)/shard_map/ppermute | solution.py:121
  75.7 1.0 collective-permute-done.13
  77.9 2.7 %all-gather = bf16[16,6,5120]{2,1,0:T(8,128)(2,1)S(1)} all-gather(bf16[16,6,2560]{2,1,0:T(8,128)(2,1)S(1)} %gather_fusion), channel_id=2, replica_groups=mesh['ctx'=16,'tp'=2] {'tp'}, dimensions={2}, use_global_device_ids=true | all-gather | bytes 1474560 | tf_op jit(solution)/shard_map/all_gather | solution.py:124
  81.1 8.9 %fusion.24 = f32[96,2048]{1,0:T(8,128)S(1)} fusion(bf16[96,5120]{1,0:T(8,128)(2,1)S(1)} %reshape.108, bf16[1,5120,2048]{2,1,0:T(8,128)(2,1)} %param.17), kind=kOutput, calls=%fused_computation.27 | convolution fusion | flops 2013265920 | bytes 22740992 | tf_op jit(solution)/shard_map/dot_general | solution.py:127
  90.0 11.1 %fusion.32 = bf16[96,2048]{1,0:T(8,128)(2,1)S(1)} fusion(bf16[96,5120]{1,0:T(8,128)(2,1)S(1)} %reshape.108, bf16[1,5120,2048]{2,1,0:T(8,128)(2,1)} %param.18, f32[96,2048]{1,0:T(8,128)S(1)} %fusion.24), kind=kOutput, calls=%fused_computation.32 | convolution fusion | flops 2014445568 | bytes 23134208 | tf_op jit(solution)/shard_map/dot_general | solution.py:128
  101.1 2.4 %all_gather.15 = bf16[96,4096]{1,0:T(8,128)(2,1)S(1)} all-gather(bf16[96,2048]{1,0:T(8,128)(2,1)S(1)} %fusion.32), channel_id=1, replica_groups=mesh['ctx'=16,'tp'=2] {'tp'}, dimensions={1}, use_global_device_ids=true | all-gather | bytes 1179648 | tf_op jit(solution)/shard_map/all_gather | solution.py:130
  103.6 3.4 %fusion.26 = bf16[96,2560]{1,0:T(8,128)(2,1)S(1)} fusion(bf16[96,4096]{1,0:T(8,128)(2,1)S(1)} %all_gather.15, bf16[1,4096,2560]{2,1,0:T(8,128)(2,1)S(1)} %bitcast.115), kind=kOutput, calls=%fused_computation.29 | convolution fusion | flops 2013511680 | bytes 22249472 | tf_op jit(solution)/shard_map/dot_general | solution.py:131
  107.0 1.0 reshape.109
  108.0 7.3 %all-to-all-start = ((bf16[16,6,2560]{2,1,0:T(8,128)(2,1)}), bf16[16,6,2560]{2,1,0:T(8,128)(2,1)S(1)}, u32[]{:S(2)}, u32[]{:S(2)}) async-start(bf16[16,6,2560]{2,1,0:T(8,128)(2,1)} %reshape.109), calls=%async_computation | async-start | bytes 1310720 | tf_op jit(solution)/shard_map/all_to_all | solution.py:135
  115.3 48.3 %all_gather.13 = bf16[1024,256]{1,0:T(8,128)(2,1)S(1)} all-gather(bf16[64,256]{1,0:T(8,128)(2,1)S(1)} %copy-done.5), channel_id=1, replica_groups=mesh['ctx'=16,'tp'=2] {'ctx'}, dimensions={0}, use_global_device_ids=true | all-gather | bytes 557056 | tf_op jit(solution)/shard_map/all_gather | solution.py:46
  163.6 6.2 %conditional.1 = ((f32[2,5,64]{2,1,0:T(8,128)S(1)}, f32[64,2,5,128]{3,0,2,1:T(8,128)S(1)})) conditional(s32[]{:T(128)} %convert_element_type.33, (f32[2,5,64]{2,1,0:T(8,128)S(1)}, f32[64,2,5,128]{3,0,2,1:T(8,128)S(1)}) %tuple.25, (s32[64]{0:T(128)S(1)}, s32[1024]{0:T(1024)S(1)}, bf16[1024,256]{1,0:T(8,128)(2,1)S(1)}, bf16[64,1280]{1,0:T(8,128)(2,1)S(1)}, ...), branch_computations={%region_2.3_spmd, %region_3.6_spmd} | conditional | flops 344295296 | bytes 22939956 | solution.py:88
  164.1 0.7 fusion
  164.8 1.5 copy-done.2
  166.3 0.8 fusion.2
  167.2 2.6 %fusion.9 = f32[64,2,5,128]{3,0,2,1:T(8,128)S(1)} fusion(f32[2,1024,64,5]{1,2,3,0:T(8,128)} %copy-done.2, f32[2,5,64]{2,1,0:T(8,128)S(1)} %broadcast_maximum_fusion, pred[64,1024]{1,0:T(8,128)(4,1)S(1)} %broadcast_compare_fusion, bf16[1024,2,128,1]{2,1,0,3:T(2,128)(2,1)S(1)} %bitcast.117, f32[64,2,5,128]{3,0,2,1:T(8,128)S(1)} %get-tuple-element.89, ...), kind=kOutput, calls=%fused_computation.10 | convolution fusion | flops 171212800 | bytes 3871744 | tf_op jit(solution)/shard_map/while/body/eval_jaxpr/cond/branch_1_fun/hgqk,khd->qhgd/dot_general | solution.py:76
  170.2 0.9 convert_element_type.35
  171.2 0.8 gather_fusion.1
  172.0 0.8 multiply_convert_fusion
  (85 shorter events, 5.0 us)
Async XLA Ops:
  0.6 2.5 %copy-start = (bf16[64,2560]{1,0:T(8,128)(2,1)S(1)}, bf16[64,2560]{1,0:T(8,128)(2,1)}, u32[]{:S(2)}) copy-start(bf16[64,2560]{1,0:T(8,128)(2,1)} %param.14) | copy-start | bytes 983044
  0.6 13.4 %copy-start.4 = (bf16[64,256]{1,0:T(8,128)(2,1)S(1)}, bf16[64,256]{1,0:T(8,128)(2,1)}, u32[]{:S(2)}) copy-start(bf16[64,256]{1,0:T(8,128)(2,1)} %param.12) | copy-start | bytes 98308
  3.8 55.8 %collective-permute-start = (bf16[1,6,2560]{2,1,0:T(8,128)(2,1)S(1)}, bf16[1,6,2560]{2,1,0:T(8,128)(2,1)S(1)}, u32[]{:S(2)}, u32[]{:S(2)}) collective-permute-start(bf16[1,6,2560]{2,1,0:T(8,128)(2,1)S(1)} %get-tuple-element.117), channel_id=1, source_target_pairs={{0,2},{2,4},{4,6},{6,8},{8,10},{10,12},{12,14},{14,16},{16,18},{18... | collective-permute-start | bytes 92168 | tf_op jit(solution)/shard_map/ppermute | solution.py:121
  6.8 52.8 %collective-permute-start.1 = (bf16[1,6,2560]{2,1,0:T(8,128)(2,1)S(1)}, bf16[1,6,2560]{2,1,0:T(8,128)(2,1)S(1)}, u32[]{:S(2)}, u32[]{:S(2)}) collective-permute-start(bf16[1,6,2560]{2,1,0:T(8,128)(2,1)S(1)} %get-tuple-element.116), channel_id=1, source_target_pairs={{0,4},{2,6},{4,8},{6,10},{8,12},{10,14},{12,16},{14,18},{16,20},{1... | collective-permute-start | bytes 92168 | tf_op jit(solution)/shard_map/ppermute | solution.py:121
  8.4 51.4 %collective-permute-start.2 = (bf16[1,6,2560]{2,1,0:T(8,128)(2,1)S(1)}, bf16[1,6,2560]{2,1,0:T(8,128)(2,1)S(1)}, u32[]{:S(2)}, u32[]{:S(2)}) collective-permute-start(bf16[1,6,2560]{2,1,0:T(8,128)(2,1)S(1)} %get-tuple-element.115), channel_id=1, source_target_pairs={{0,6},{2,8},{4,10},{6,12},{8,14},{10,16},{12,18},{14,20},{16,22},{... | collective-permute-start | bytes 92168 | tf_op jit(solution)/shard_map/ppermute | solution.py:121
  10.8 49.2 %collective-permute-start.3 = (bf16[1,6,2560]{2,1,0:T(8,128)(2,1)S(1)}, bf16[1,6,2560]{2,1,0:T(8,128)(2,1)S(1)}, u32[]{:S(2)}, u32[]{:S(2)}) collective-permute-start(bf16[1,6,2560]{2,1,0:T(8,128)(2,1)S(1)} %get-tuple-element.114), channel_id=1, source_target_pairs={{0,8},{2,10},{4,12},{6,14},{8,16},{10,18},{12,20},{14,22},{16,24},... | collective-permute-start | bytes 92168 | tf_op jit(solution)/shard_map/ppermute | solution.py:121
  12.4 51.3 %collective-permute-start.4 = (bf16[1,6,2560]{2,1,0:T(8,128)(2,1)S(1)}, bf16[1,6,2560]{2,1,0:T(8,128)(2,1)S(1)}, u32[]{:S(2)}, u32[]{:S(2)}) collective-permute-start(bf16[1,6,2560]{2,1,0:T(8,128)(2,1)S(1)} %get-tuple-element.113), channel_id=1, source_target_pairs={{0,10},{2,12},{4,14},{6,16},{8,18},{10,20},{12,22},{14,24},{16,26}... | collective-permute-start | bytes 92168 | tf_op jit(solution)/shard_map/ppermute | solution.py:121
  59.6 7.8 %collective-permute-start.5 = (bf16[1,6,2560]{2,1,0:T(8,128)(2,1)S(1)}, bf16[1,6,2560]{2,1,0:T(8,128)(2,1)S(1)}, u32[]{:S(2)}, u32[]{:S(2)}) collective-permute-start(bf16[1,6,2560]{2,1,0:T(8,128)(2,1)S(1)} %get-tuple-element.112), channel_id=1, source_target_pairs={{0,12},{2,14},{4,16},{6,18},{8,20},{10,22},{12,24},{14,26},{16,28}... | collective-permute-start | bytes 92168 | tf_op jit(solution)/shard_map/ppermute | solution.py:121
  59.7 7.8 %collective-permute-start.6 = (bf16[1,6,2560]{2,1,0:T(8,128)(2,1)S(1)}, bf16[1,6,2560]{2,1,0:T(8,128)(2,1)S(1)}, u32[]{:S(2)}, u32[]{:S(2)}) collective-permute-start(bf16[1,6,2560]{2,1,0:T(8,128)(2,1)S(1)} %get-tuple-element.111), channel_id=1, source_target_pairs={{0,14},{2,16},{4,18},{6,20},{8,22},{10,24},{12,26},{14,28},{16,30}... | collective-permute-start | bytes 92168 | tf_op jit(solution)/shard_map/ppermute | solution.py:121
  59.8 10.2 %collective-permute-start.7 = (bf16[1,6,2560]{2,1,0:T(8,128)(2,1)S(1)}, bf16[1,6,2560]{2,1,0:T(8,128)(2,1)S(1)}, u32[]{:S(2)}, u32[]{:S(2)}) collective-permute-start(bf16[1,6,2560]{2,1,0:T(8,128)(2,1)S(1)} %get-tuple-element.110), channel_id=1, source_target_pairs={{0,16},{2,18},{4,20},{6,22},{8,24},{10,26},{12,28},{14,30},{16,0},... | collective-permute-start | bytes 92168 | tf_op jit(solution)/shard_map/ppermute | solution.py:121
  60.0 12.7 %collective-permute-start.8 = (bf16[1,6,2560]{2,1,0:T(8,128)(2,1)S(1)}, bf16[1,6,2560]{2,1,0:T(8,128)(2,1)S(1)}, u32[]{:S(2)}, u32[]{:S(2)}) collective-permute-start(bf16[1,6,2560]{2,1,0:T(8,128)(2,1)S(1)} %get-tuple-element.109), channel_id=1, source_target_pairs={{0,18},{2,20},{4,22},{6,24},{8,26},{10,28},{12,30},{14,0},{16,2},{... | collective-permute-start | bytes 92168 | tf_op jit(solution)/shard_map/ppermute | solution.py:121
  63.6 9.6 %collective-permute-start.9 = (bf16[1,6,2560]{2,1,0:T(8,128)(2,1)S(1)}, bf16[1,6,2560]{2,1,0:T(8,128)(2,1)S(1)}, u32[]{:S(2)}, u32[]{:S(2)}) collective-permute-start(bf16[1,6,2560]{2,1,0:T(8,128)(2,1)S(1)} %get-tuple-element.108), channel_id=1, source_target_pairs={{0,20},{2,22},{4,24},{6,26},{8,28},{10,30},{12,0},{14,2},{16,4},{1... | collective-permute-start | bytes 92168 | tf_op jit(solution)/shard_map/ppermute | solution.py:121
  67.4 8.3 %collective-permute-start.10 = (bf16[1,6,2560]{2,1,0:T(8,128)(2,1)S(1)}, bf16[1,6,2560]{2,1,0:T(8,128)(2,1)S(1)}, u32[]{:S(2)}, u32[]{:S(2)}) collective-permute-start(bf16[1,6,2560]{2,1,0:T(8,128)(2,1)S(1)} %get-tuple-element.107), channel_id=1, source_target_pairs={{0,22},{2,24},{4,26},{6,28},{8,30},{10,0},{12,2},{14,4},{16,6},{18... | collective-permute-start | bytes 92168 | tf_op jit(solution)/shard_map/ppermute | solution.py:121
  67.5 8.2 %collective-permute-start.11 = (bf16[1,6,2560]{2,1,0:T(8,128)(2,1)S(1)}, bf16[1,6,2560]{2,1,0:T(8,128)(2,1)S(1)}, u32[]{:S(2)}, u32[]{:S(2)}) collective-permute-start(bf16[1,6,2560]{2,1,0:T(8,128)(2,1)S(1)} %get-tuple-element.106), channel_id=1, source_target_pairs={{0,24},{2,26},{4,28},{6,30},{8,0},{10,2},{12,4},{14,6},{16,8},{18,... | collective-permute-start | bytes 92168 | tf_op jit(solution)/shard_map/ppermute | solution.py:121
  70.0 5.7 %collective-permute-start.12 = (bf16[1,6,2560]{2,1,0:T(8,128)(2,1)S(1)}, bf16[1,6,2560]{2,1,0:T(8,128)(2,1)S(1)}, u32[]{:S(2)}, u32[]{:S(2)}) collective-permute-start(bf16[1,6,2560]{2,1,0:T(8,128)(2,1)S(1)} %get-tuple-element.105), channel_id=1, source_target_pairs={{0,26},{2,28},{4,30},{6,0},{8,2},{10,4},{12,6},{14,8},{16,10},{18,... | collective-permute-start | bytes 92168 | tf_op jit(solution)/shard_map/ppermute | solution.py:121
  72.7 4.0 %collective-permute-start.13 = (bf16[1,6,2560]{2,1,0:T(8,128)(2,1)S(1)}, bf16[1,6,2560]{2,1,0:T(8,128)(2,1)S(1)}, u32[]{:S(2)}, u32[]{:S(2)}) collective-permute-start(bf16[1,6,2560]{2,1,0:T(8,128)(2,1)S(1)} %get-tuple-element.104), channel_id=1, source_target_pairs={{0,28},{2,30},{4,0},{6,2},{8,4},{10,6},{12,8},{14,10},{16,12},{18,... | collective-permute-start | bytes 92168 | tf_op jit(solution)/shard_map/ppermute | solution.py:121
  73.3 4.0 %collective-permute-start.14 = (bf16[1,6,2560]{2,1,0:T(8,128)(2,1)S(1)}, bf16[1,6,2560]{2,1,0:T(8,128)(2,1)S(1)}, u32[]{:S(2)}, u32[]{:S(2)}) collective-permute-start(bf16[1,6,2560]{2,1,0:T(8,128)(2,1)S(1)} %get-tuple-element.103), channel_id=1, source_target_pairs={{0,30},{2,0},{4,2},{6,4},{8,6},{10,8},{12,10},{14,12},{16,14},{18,... | collective-permute-start | bytes 92168 | tf_op jit(solution)/shard_map/ppermute | solution.py:121
  81.0 22.5 %slice-start = ((s8[20971520]{0:T(1024)(128)(4,1)}), s8[4194304]{0:T(1024)(128)(4,1)S(1)}, s32[]{:S(2)}) async-start(s8[20971520]{0:T(1024)(128)(4,1)} %bitcast.114), calls=%async_computation.1 | async-start | bytes 8388608
  81.0 22.5 %slice-start.1 = ((s8[20971520]{0:T(1024)(128)(4,1)}), s8[4194304]{0:T(1024)(128)(4,1)S(1)}, s32[]{:S(2)}) async-start(s8[20971520]{0:T(1024)(128)(4,1)} %bitcast.114), calls=%async_computation.2 | async-start | bytes 8388608
  81.1 22.5 %slice-start.2 = ((s8[20971520]{0:T(1024)(128)(4,1)}), s8[4194304]{0:T(1024)(128)(4,1)S(1)}, s32[]{:S(2)}) async-start(s8[20971520]{0:T(1024)(128)(4,1)} %bitcast.114), calls=%async_computation.3 | async-start | bytes 8388608
  90.0 13.5 %slice-start.3 = ((s8[20971520]{0:T(1024)(128)(4,1)}), s8[4194304]{0:T(1024)(128)(4,1)S(1)}, s32[]{:S(2)}) async-start(s8[20971520]{0:T(1024)(128)(4,1)} %bitcast.114), calls=%async_computation.4 | async-start | bytes 8388608
  90.0 13.5 %slice-start.4 = ((s8[20971520]{0:T(1024)(128)(4,1)}), s8[4194304]{0:T(1024)(128)(4,1)S(1)}, s32[]{:S(2)}) async-start(s8[20971520]{0:T(1024)(128)(4,1)} %bitcast.114), calls=%async_computation.5 | async-start | bytes 8388608
  103.6 11.8 %copy-start.5 = (bf16[64,256]{1,0:T(8,128)(2,1)S(1)}, bf16[64,256]{1,0:T(8,128)(2,1)}, u32[]{:S(2)}) copy-start(bf16[64,256]{1,0:T(8,128)(2,1)} %param.13) | copy-start | bytes 98308
  107.0 56.6 %copy-start.3 = (bf16[64,1280]{1,0:T(8,128)(2,1)S(1)}, bf16[64,1280]{1,0:T(8,128)(2,1)}, u32[]{:S(2)}) copy-start(bf16[64,1280]{1,0:T(8,128)(2,1)} %param.11) | copy-start | bytes 491524
  108.0 63.1 %all-to-all-start = ((bf16[16,6,2560]{2,1,0:T(8,128)(2,1)}), bf16[16,6,2560]{2,1,0:T(8,128)(2,1)S(1)}, u32[]{:S(2)}, u32[]{:S(2)}) async-start(bf16[16,6,2560]{2,1,0:T(8,128)(2,1)} %reshape.109), calls=%async_computation | async-start | bytes 1310720 | tf_op jit(solution)/shard_map/all_to_all | solution.py:135
  163.6 7.4 %copy-start.6 = (s32[64,1]{0,1:T(1,128)S(1)}, s32[64,1]{0,1:T(1,128)}, u32[]{:S(2)}) copy-start(s32[64,1]{0,1:T(1,128)} %param.15) | copy-start | bytes 772
  164.8 1.5 copy-start.2
  171.0 1.8 %copy-start.1 = (bf16[64,2560]{1,0:T(8,128)(2,1)S(1)}, bf16[64,2560]{1,0:T(8,128)(2,1)}, u32[]{:S(2)}) copy-start(bf16[64,2560]{1,0:T(8,128)(2,1)} %param.14) | copy-start | bytes 983044
  171.2 0.8 copy-start.7
